TPU v7x, 32 devices: a whole 2x2x4 slice. The times are simulated.
32 devices in a mesh: lat: 16 (over z, y, x), ord: 2 (over core).
Axes of the slice: x: 2, y: 2, z: 4, core: 2. Of those that a mesh axis runs over, the one named last changes fastest.
Arguments:
- pressure: bfloat16 [2, 128, 5760], P(None, 'lat', 'ord'), may hold values from -6 to 6
- tables: bfloat16 [512, 128, 2048], P('ord', 'lat'), may hold values from -6 to 6
- quad_weight: float32 [128], replicated, may hold values from 0.5 to 2
- love_number: float32 [2048], replicated, may hold values from -0.5 to 0
- order_list: int32 [512], replicated, may hold values from 0 to 511, each once
- cycle_list: int32 [128], P('lat'), may hold values from 0 to 127, each once
Outputs:
- spectrum: float32 [2, 512, 2048], P(None, 'ord', 'lat')
- load_field: float32 [2, 128, 5760], P(None, 'lat', 'ord')
Inputs may be any that keep to these rules, and one draw needn't show every extreme that they name: `order_list`: every order from 0 to 511 stands in exactly one slot. `cycle_list`: every northern cycle from 0 to 127 stands in exactly one slot; the same slot of the southern half holds its mirror cycle.
All inputs are finite; a program needn't handle non-finite values.
Results may differ from a plain program's by a relative error of at most 0.0055.
Values may be sent and summed in bfloat16 or wider, within the bound.
A program may use at most 64 MiB of HBM per device.

v0:
```python
import functools
import math

import jax
import jax.numpy as jnp
from jax import lax
from jax.experimental import pallas as pl
from jax.experimental.pallas import tpu as pltpu
from jax.sharding import PartitionSpec as P

DENSITY_RATIO = 3.0 * 1025.0 / 5517.0
LANES = 128
GROUPS = 8
STAGGER = 2
MESH = pl.DeviceIdType.MESH
NT = (((1,), (1,)), ((), ()))
F32 = jnp.float32
BF16 = jnp.bfloat16


def bit_orders(bits):
    base = list(range(bits))
    if bits < 3:
        return [base] * GROUPS
    a = base
    b = [1, 0] + base[2:]
    c = [2, 0, 1] + base[3:]
    d = [2, 1, 0] + base[3:]
    return [a, b, c, a, b, d, a, b]


def permuted(index, order):
    bits = len(order)
    return sum(((index // 2**b) % 2) * 2 ** (bits - 1 - at) for at, b in enumerate(order))


def kernel(
    n, no, cycles, half_lon,
    press_ref, tables_ref, cos_q, sin_q, cos_r, sin_r, orders_ref, fold_ref, sel_ref, love_ref,
    spec_ref, field_ref,
    tab, wave, gathered, lhs, part, landed, scaled, picked, out_piece, in_piece,
    tab_sem, press_sem, rs_sem, ag_sem, field_sem,
):
    bits = n.bit_length() - 1
    me = lax.axis_index("lat")
    core = lax.axis_index("ord")
    local_orders = orders_ref.shape[0]
    degrees = tables_ref.shape[1]
    share = degrees // n
    go = local_orders // GROUPS
    rows_g = go * cycles
    blocks = max(1, min(n, 1024 // share))
    width = blocks * share
    orders_of = bit_orders(bits)
    lon_pad = wave.shape[3]

    barrier = pltpu.get_barrier_semaphore()
    partners = []
    for b in range(bits):
        mine = (me // 2**b) % 2
        partners.append(me + (1 - 2 * mine) * 2**b)
    peers = [lax.rem(core + i, no) for i in range(1, no)]
    for partner in partners:
        pl.semaphore_signal(barrier, inc=1, device_id=(partner, core), device_id_type=MESH)
    for peer in peers:
        pl.semaphore_signal(barrier, inc=1, device_id=(me, peer), device_id_type=MESH)

    tab_copies = []
    for g in range(GROUPS):
        rows = pl.ds(g * rows_g, rows_g)
        copy = pltpu.make_async_copy(tables_ref.at[rows], tab.at[rows], tab_sem.at[g])
        copy.start()
        tab_copies.append(copy)

    pl.semaphore_wait(barrier, bits + no - 1)
    press_copies = []
    for i, peer in enumerate(peers):
        copy = pltpu.make_async_remote_copy(
            src_ref=press_ref,
            dst_ref=gathered.at[i],
            send_sem=press_sem.at[0, i],
            recv_sem=press_sem.at[1, i],
            device_id=(me, peer),
            device_id_type=MESH,
        )
        copy.start()
        press_copies.append(copy)

    def make_wave(p, carry):
        for q in range(lon_pad // LANES):
            cq = cos_q[p, :, q : q + 1]
            sq = sin_q[p, :, q : q + 1]
            cols = slice(q * LANES, (q + 1) * LANES)
            wave[p, 0, :, cols] = (cq * cos_r[...] - sq * sin_r[...]).astype(BF16)
            wave[p, 1, :, cols] = (sq * cos_r[...] + cq * sin_r[...]).astype(BF16)
        return carry

    lax.fori_loop(0, no, make_wave, 0)

    sums = [jnp.zeros((local_orders, press_ref.shape[0]), F32) for _ in range(2)]
    for i in range(no):
        if i > 0:
            press_copies[i - 1].wait()
        origin = lax.rem(core + no - i, no)
        rows = press_ref[...] if i == 0 else gathered[i - 1]
        for t in range(2):
            sums[t] = sums[t] + lax.dot_general(wave[origin, t], rows, NT, preferred_element_type=F32)

    col = lax.broadcasted_iota(jnp.int32, (local_orders, rows_g), 1) // cycles
    row = lax.broadcasted_iota(jnp.int32, (local_orders, rows_g), 0) % go
    diagonal = row == col
    for f in range(2):
        for t in range(2):
            value = lax.dot_general(
                sums[t], fold_ref[2 * f + t], (((1,), (0,)), ((), ())),
                precision=lax.Precision.HIGHEST, preferred_element_type=F32,
            )
            lhs[2 * f + t] = jnp.where(diagonal, value, 0.0)

    def parity(g, first):
        degree = first + lax.broadcasted_iota(jnp.int32, (go, width), 1)
        order = orders_ref[g * go : (g + 1) * go, :]
        return (degree + order) & 1 == 0, degree >= order

    def region(g, k):
        base = 0
        for at in range(k):
            base = base + ((me // 2 ** orders_of[g][at]) % 2) * (n >> (at + 1))
        return base

    def analyse(g):
        tab_copies[g].wait()
        left = jnp.concatenate([lhs[c, g * go : (g + 1) * go, :] for c in range(4)], 0).astype(BF16)

        def chunk(i, carry):
            first = pl.multiple_of(i * width, width)
            product = jnp.dot(
                left, tab[g * rows_g : (g + 1) * rows_g, pl.ds(first, width)], preferred_element_type=F32
            )
            even, present = parity(g, first)
            real = jnp.where(present, jnp.where(even, product[:go], product[2 * go : 3 * go]), 0.0)
            imag = jnp.where(present, jnp.where(even, product[go : 2 * go], product[3 * go :]), 0.0)
            value = jnp.concatenate([real, imag], 0).astype(BF16)
            for j in range(blocks):
                to = permuted(i * blocks + j, orders_of[g])
                part[g, to] = value[:, j * share : (j + 1) * share]
            return carry

        lax.fori_loop(0, degrees // width, chunk, 0)

    reduce_copies = {}
    gather_copies = {}

    def send_reduce(g, k):
        h = n >> (k + 1)
        b = orders_of[g][k]
        mine = (me // 2**b) % 2
        copy = pltpu.make_async_remote_copy(
            src_ref=part.at[g, pl.ds(region(g, k) + (1 - mine) * h, h)],
            dst_ref=landed.at[g, pl.ds(n - (n >> k), h)],
            send_sem=rs_sem.at[0, g, k],
            recv_sem=rs_sem.at[1, g, k],
            device_id=(partners[b], core),
            device_id_type=MESH,
        )
        copy.start()
        reduce_copies[g, k] = copy

    def take_reduce(g, k):
        h = n >> (k + 1)
        reduce_copies[g, k].wait_recv()
        keep = region(g, k + 1)
        off = n - (n >> k)
        if k < bits - 1:

            def add(i, carry):
                part[g, keep + i] = (
                    part[g, keep + i].astype(F32) + landed[g, off + i].astype(F32)
                ).astype(BF16)
                return carry

            lax.fori_loop(0, h, add, 0, unroll=min(h, 4))
            send_reduce(g, k + 1)
            return
        total = part[g, keep].astype(F32) + landed[g, off].astype(F32)
        spec_ref[0, g * go : (g + 1) * go, :] = total[:go]
        spec_ref[1, g * go : (g + 1) * go, :] = total[go:]
        scaled[g, keep] = (love_ref[...] * total).astype(BF16)
        send_gather(g, bits - 1)

    def send_gather(g, k):
        h = n >> (k + 1)
        b = orders_of[g][k]
        mine = pl.ds(region(g, k + 1), h)
        copy = pltpu.make_async_remote_copy(
            src_ref=scaled.at[g, mine],
            dst_ref=scaled.at[g, mine],
            send_sem=ag_sem.at[0, g, k],
            recv_sem=ag_sem.at[1, g, k],
            device_id=(partners[b], core),
            device_id_type=MESH,
        )
        copy.start()
        gather_copies[g, k] = copy

    def take_gather(g, k):
        gather_copies[g, k].wait_recv()
        if k > 0:
            send_gather(g, k - 1)

    def synthesise(g):
        def chunk(i, total):
            first = pl.multiple_of(i * width, width)
            even, _ = parity(g, first)
            pieces = [scaled[g, permuted(i * blocks + j, orders_of[g])] for j in range(blocks)]
            both = jnp.concatenate(pieces, 1).astype(F32)
            real, imag = both[:go], both[go:]
            stacked = jnp.concatenate(
                [real, imag, jnp.where(even, real, -real), jnp.where(even, imag, -imag)], 0
            ).astype(BF16)
            return total + lax.dot_general(
                stacked, tab[g * rows_g : (g + 1) * rows_g, pl.ds(first, width)], NT,
                preferred_element_type=F32,
            )

        total = lax.fori_loop(0, degrees // width, chunk, jnp.zeros((4 * go, rows_g), F32))
        total = total * (1.0 / math.sqrt(degrees))
        keep = diagonal[:go]
        for c in range(4):
            picked[c, g * go : (g + 1) * go, :] = jnp.where(keep, total[c * go : (c + 1) * go], 0.0)

    steps = []
    for g in range(GROUPS):
        steps.append((g, g, lambda g=g: (analyse(g), send_reduce(g, 0))))
        for k in range(bits):
            steps.append((g + STAGGER * (k + 1), g, lambda g=g, k=k: take_reduce(g, k)))
        for i, k in enumerate(reversed(range(bits))):
            steps.append((g + STAGGER * (bits + i + 1), g, lambda g=g, k=k: take_gather(g, k)))
        steps.append((g + STAGGER * 2 * bits + 1, g, lambda g=g: synthesise(g)))
    for _, _, step in sorted(steps, key=lambda s: (s[0], s[1])):
        step()

    signal = []
    for t in range(2):
        north = lax.dot_general(sel_ref[0], picked[t].astype(BF16), NT, preferred_element_type=F32)
        south = lax.dot_general(sel_ref[1], picked[2 + t].astype(BF16), NT, preferred_element_type=F32)
        signal.append((north + south).astype(BF16))
    signal[1] = -signal[1]

    def piece(p):
        total = jnp.dot(signal[0], wave[p, 0], preferred_element_type=F32)
        return total + jnp.dot(signal[1], wave[p, 1], preferred_element_type=F32)

    field_copies = []
    for i, peer in enumerate(peers):
        out_piece[i] = piece(peer)
        copy = pltpu.make_async_remote_copy(
            src_ref=out_piece.at[i],
            dst_ref=in_piece.at[i],
            send_sem=field_sem.at[0, i],
            recv_sem=field_sem.at[1, i],
            device_id=(me, peer),
            device_id_type=MESH,
        )
        copy.start()
        field_copies.append(copy)
    total = piece(core)
    for i, copy in enumerate(field_copies):
        copy.wait_recv()
        total = total + in_piece[i]
    field_ref[...] = total[:, :half_lon] * (1.0 / math.sqrt(local_orders * no))
    for copy in list(reduce_copies.values()) + list(gather_copies.values()) + field_copies:
        copy.wait_send()


def cos_sin(phase, period):
    angle = (phase % period).astype(F32) * (2.0 * math.pi / period)
    return jnp.cos(angle), jnp.sin(angle)


def per_device(n, no, pressure, tables, quad_weight, love_number, order_list, cycle_list):
    cycles = pressure.shape[1]
    lon_local = pressure.shape[2]
    local_orders = tables.shape[0]
    degrees = tables.shape[2]
    half_total = quad_weight.shape[0]
    period = lon_local * no
    bits = n.bit_length() - 1
    share = degrees // n
    go = local_orders // GROUPS
    rows_g = go * cycles
    tiles = -(-lon_local // LANES)
    lon_pad = tiles * LANES
    my_orders = lax.dynamic_slice_in_dim(
        order_list, lax.axis_index("ord") * local_orders, local_orders
    )
    rows = jnp.pad(pressure.reshape(2 * cycles, lon_local), ((0, 0), (0, lon_pad - lon_local)))
    starts = (
        lon_local * jnp.arange(no, dtype=jnp.int32)[:, None]
        + LANES * jnp.arange(tiles, dtype=jnp.int32)[None, :]
    )
    cos_q, sin_q = cos_sin(my_orders[None, :, None] * starts[:, None, :], period)
    cos_r, sin_r = cos_sin(my_orders[:, None] * jnp.arange(LANES, dtype=jnp.int32)[None, :], period)
    matches = cycle_list[:, None] == jnp.arange(half_total, dtype=jnp.int32)[None, :]
    weight = jnp.sum(jnp.where(matches, quad_weight[None, :], 0.0), axis=1) * (
        1.0 / math.sqrt(half_total)
    )
    eye = jnp.tile(jnp.eye(cycles, dtype=F32), (1, go))
    spread = weight[:, None] * eye * (1.0 / math.sqrt(period))
    fold = jnp.stack(
        [
            jnp.concatenate([spread, spread], 0),
            -jnp.concatenate([spread, spread], 0),
            jnp.concatenate([spread, -spread], 0),
            -jnp.concatenate([spread, -spread], 0),
        ]
    )
    zero = jnp.zeros_like(eye)
    sel = jnp.stack([jnp.concatenate([eye, zero], 0), jnp.concatenate([zero, eye], 0)]).astype(BF16)
    love = (DENSITY_RATIO * (1.0 + love_number))[None, :]
    love = lax.dynamic_slice_in_dim(love, lax.axis_index("lat") * share, share, 1)

    vmem = pl.BlockSpec(memory_space=pltpu.VMEM)
    spectrum, field = pl.pallas_call(
        functools.partial(kernel, n, no, cycles, lon_local),
        out_shape=(
            jax.ShapeDtypeStruct((2, local_orders, share), F32),
            jax.ShapeDtypeStruct((2 * cycles, lon_local), F32),
        ),
        in_specs=[vmem, pl.BlockSpec(memory_space=pl.ANY)] + [vmem] * 8,
        out_specs=(vmem, vmem),
        scratch_shapes=[
            pltpu.VMEM((local_orders * cycles, degrees), BF16),
            pltpu.VMEM((no, 2, local_orders, lon_pad), BF16),
            pltpu.VMEM((no - 1, 2 * cycles, lon_pad), BF16),
            pltpu.VMEM((4, local_orders, rows_g), F32),
            pltpu.VMEM((GROUPS, n, 2 * go, share), BF16),
            pltpu.VMEM((GROUPS, n, 2 * go, share), BF16),
            pltpu.VMEM((GROUPS, n, 2 * go, share), BF16),
            pltpu.VMEM((4, local_orders, rows_g), F32),
            pltpu.VMEM((no - 1, 2 * cycles, lon_pad), F32),
            pltpu.VMEM((no - 1, 2 * cycles, lon_pad), F32),
            pltpu.SemaphoreType.DMA((GROUPS,)),
            pltpu.SemaphoreType.DMA((2, no - 1)),
            pltpu.SemaphoreType.DMA((2, GROUPS, bits)),
            pltpu.SemaphoreType.DMA((2, GROUPS, bits)),
            pltpu.SemaphoreType.DMA((2, no - 1)),
        ],
        compiler_params=pltpu.CompilerParams(
            collective_id=0, has_side_effects=True, vmem_limit_bytes=56 * 1024 * 1024
        ),
    )(
        rows, tables.reshape(local_orders * cycles, degrees), cos_q, sin_q, cos_r, sin_r,
        my_orders[:, None], fold, sel, love,
    )
    return spectrum, field.reshape(2, cycles, lon_local)


def solution(mesh):
    placed = (P(None, "lat", "ord"), P("ord", "lat", None), P(), P(), P(), P("lat"))
    return jax.shard_map(
        functools.partial(per_device, mesh.shape["lat"], mesh.shape["ord"]),
        mesh=mesh,
        in_specs=placed,
        out_specs=(P(None, "ord", "lat"), P(None, "lat", "ord")),
        check_vma=False,
    )
```

profile of v0, /device:TPU:0, one launch (start us, length us, event | category | flops | bytes accessed | tf_op | source)
XLA Modules:
  0.0 81.2 jit_solution(9832737109561896193)
XLA Ops:
  0.6 1.3 %fusion.20.love_ref = f32[1,128]{1,0:T(1,128)} fusion(f32[2048]{0:T(1024)} %param.9, s32[]{:T(128)S(6)} %select_n.27), kind=kLoop, calls=%fused_computation.40 | loop fusion | flops 256 | bytes 1028 | tf_op jit(solution)/shard_map/dynamic_slice | solution.py:321
  1.9 0.8 dynamic_slice.6
  2.7 0.9 %select_reduce_fusion = f32[8]{0:T(128)S(1)} fusion(f32[128]{0:T(128)} %param.8, s32[8]{0:T(128)} %param.11), kind=kLoop, calls=%fused_computation.32 | loop fusion | flops 3064 | bytes 576 | tf_op jit(solution)/shard_map/reduce_sum | solution.py:305
  3.5 0.1 broadcast_add_fusion
  3.6 1.5 %pad.8.press_ref = bf16[16,2944]{1,0:T(8,128)(2,1)} pad(bf16[16,2880]{1,0:T(8,128)(2,1)} %bitcast.20, bf16[]{:T(256)} %constant.16.clone.1), padding=0_0x0_64 | pad | bytes 186370 | tf_op jit(solution)/shard_map/jit(_pad)/pad | solution.py:297
  5.2 0.1 tile.18
  5.3 0.1 fusion.21
  5.4 0.6 pad_maximum_fusion.5.sel_ref
  6.0 0.6 pad_maximum_fusion.fold_ref
  6.6 0.8 copy.9.orders_ref
  7.4 1.3 %fusion.11 = (f32[256,128]{1,0:T(8,128)}, f32[256,128]{1,0:T(8,128)}) fusion(s32[256]{0:T(256)S(1)} %dynamic_slice.6), kind=kLoop, calls=%fused_computation.15 | loop fusion | flops 294912 | bytes 263168 | tf_op jit(solution)/shard_map/sin | solution.py:278
  8.8 2.0 %fusion.4 = (f32[2,256,23]{2,1,0:T(8,128)}, f32[2,256,23]{2,1,0:T(8,128)}) fusion(s32[2,23]{1,0:T(2,128)S(1)} %broadcast_add_fusion, s32[256]{0:T(256)S(1)} %dynamic_slice.6), kind=kLoop, calls=%fused_computation.6 | loop fusion | flops 105984 | bytes 95416 | tf_op jit(solution)/shard_map/sin | solution.py:278
  10.7 67.2 %shard_map.77 = (f32[2,256,128]{2,1,0:T(8,128)}, f32[16,2880]{1,0:T(8,128)}) custom-call(bf16[16,2944]{1,0:T(8,128)(2,1)} %pad.8.press_ref, bf16[2048,2048]{1,0:T(8,128)(2,1)} %bitcast.17, f32[2,256,23]{2,1,0:T(8,128)} %get-tuple-element.16.cos_q, f32[2,256,23]{2,1,0:T(8,128)} %get-tuple-element.15.sin_q, f32[256,128]{1,0:T(8,128)} %get-tuple-element.18.cos_r, ...), custom_call_target="tpu_custom_call" | custom-call | tf_op jit(solution)/shard_map/pallas_call | solution.py:324
  77.9 1.7 %copy.12 = f32[2,256,128]{2,1,0:T(8,128)} copy(f32[2,256,128]{2,1,0:T(8,128)} %get-tuple-element.21) | data formatting | bytes 524288
  79.6 1.6 %copy.13 = f32[2,8,2880]{2,1,0:T(8,128)} copy(f32[2,8,2880]{2,1,0:T(8,128)} %bitcast.18) | data formatting | bytes 368640
  (9 shorter events, 0.0 us)
where the time goes:
time: 81.5 us; the launch traced here: 81.2 us
  Pallas kernels  67.2 us (82%)
  other arithmetic  6.84 us (8%)
  local copies, waits for them, and re-layouts  6.5 us (8%)
    pallas_call x1, Pallas kernels, per_device(): pl.pallas_call(functools.partial(kernel, n, no, cycles, lon_local), out_s...  67.2 us
    sin x2, other arithmetic, cos_sin(): return (jnp.cos(angle), jnp.sin(angle))  3.3 us
    unnamed x2, local copies, waits for them, and re-layouts  3.28 us

commit v1 on v0

v1 whole, which is shorter than its diff:
```python
import functools
import math

import jax
import jax.numpy as jnp
from jax import lax
from jax.experimental import pallas as pl
from jax.experimental.pallas import tpu as pltpu
from jax.sharding import PartitionSpec as P

DENSITY_RATIO = 3.0 * 1025.0 / 5517.0
LANES = 128
GROUPS = 8
SETS = 2
STAGGER = 4
MESH = pl.DeviceIdType.MESH
NT = (((1,), (1,)), ((), ()))
F32 = jnp.float32
BF16 = jnp.bfloat16


def bit_orders(bits):
    base = list(range(bits))
    if bits < 3:
        return [base] * GROUPS
    a = base
    b = [1, 0] + base[2:]
    c = [2, 0, 1] + base[3:]
    d = [2, 1, 0] + base[3:]
    return [a, b, c, a, b, d, a, b]


def permuted(index, order):
    bits = len(order)
    return sum(((index // 2**b) % 2) * 2 ** (bits - 1 - at) for at, b in enumerate(order))


def cos_sin(count, period):
    turns = count - jnp.floor(count * (1.0 / period)) * period
    quarter = jnp.floor(turns * (4.0 / period) + 0.5)
    x = (turns - quarter * (period / 4.0)) * (2.0 * math.pi / period)
    y = x * x
    s = x * (1.0 + y * (-1.0 / 6 + y * (1.0 / 120 + y * (-1.0 / 5040 + y * (1.0 / 362880)))))
    c = 1.0 + y * (-0.5 + y * (1.0 / 24 + y * (-1.0 / 720 + y * (1.0 / 40320))))
    which = quarter.astype(jnp.int32) & 3
    swap = (which & 1) == 1
    cos = jnp.where(swap, s, c)
    sin = jnp.where(swap, c, s)
    return (
        jnp.where((which == 1) | (which == 2), -cos, cos),
        jnp.where(which >= 2, -sin, sin),
    )


def kernel(
    n, no,
    press_ref, tables_ref, quad_ref, love_ref, order_ref, cycle_ref,
    spec_ref, field_ref,
    tab, wave, gathered, padded, cos_q, sin_q, cos_r, sin_r, orders_ref, lhs, part, landed, scaled,
    picked, own_piece, out_piece, in_piece,
    tab_sem, press_sem, rs_sem, ag_sem, field_sem,
):
    bits = n.bit_length() - 1
    me = lax.axis_index("lat")
    core = lax.axis_index("ord")
    cycles = press_ref.shape[1]
    lon_local = press_ref.shape[2]
    local_orders = orders_ref.shape[0]
    degrees = tables_ref.shape[1]
    share = degrees // n
    go = local_orders // GROUPS
    set_orders = local_orders // SETS
    rows_g = go * cycles
    blocks = max(1, min(n, 1024 // share))
    width = blocks * share
    orders_of = bit_orders(bits)
    lon_pad = wave.shape[3]
    period = lon_local * no

    barrier = pltpu.get_barrier_semaphore()
    partners = []
    for b in range(bits):
        mine = (me // 2**b) % 2
        partners.append(me + (1 - 2 * mine) * 2**b)
    peers = [lax.rem(core + i, no) for i in range(1, no)]
    for partner in partners:
        pl.semaphore_signal(barrier, inc=1, device_id=(partner, core), device_id_type=MESH)
    for peer in peers:
        pl.semaphore_signal(barrier, inc=1, device_id=(me, peer), device_id_type=MESH)

    tab_copies = []
    for g in range(GROUPS):
        rows = pl.ds(g * rows_g, rows_g)
        copy = pltpu.make_async_copy(tables_ref.at[rows], tab.at[rows], tab_sem.at[g])
        copy.start()
        tab_copies.append(copy)

    pl.semaphore_wait(barrier, bits + no - 1)
    press_copies = []
    for i, peer in enumerate(peers):
        copy = pltpu.make_async_remote_copy(
            src_ref=press_ref,
            dst_ref=gathered.at[i],
            send_sem=press_sem.at[0, i],
            recv_sem=press_sem.at[1, i],
            device_id=(me, peer),
            device_id_type=MESH,
        )
        copy.start()
        press_copies.append(copy)

    shape = (local_orders, order_ref.shape[1])
    slot = core * local_orders + lax.broadcasted_iota(jnp.int32, shape, 0)
    hit = slot == lax.broadcasted_iota(jnp.int32, shape, 1)
    order_col = jnp.sum(jnp.where(hit, order_ref[...].astype(F32), 0.0), axis=1, keepdims=True)
    orders_ref[...] = order_col.astype(jnp.int32)
    lane = lax.broadcasted_iota(jnp.int32, (local_orders, LANES), 1)
    cos_r[...], sin_r[...] = cos_sin(order_col * lane.astype(F32), period)
    for p in range(no):
        start = (p * lon_local + LANES * lane).astype(F32)
        cos_q[p], sin_q[p] = cos_sin(order_col * start, period)

    fold_shape = (2 * cycles, rows_g)
    fold_row = lax.broadcasted_iota(jnp.int32, fold_shape, 0)
    fold_col = lax.broadcasted_iota(jnp.int32, fold_shape, 1) % cycles
    spread = jnp.zeros(fold_shape, F32)
    quad_lane = lax.broadcasted_iota(jnp.int32, quad_ref.shape, 1)
    for j in range(cycles):
        weight = jnp.sum(
            jnp.where(quad_lane == cycle_ref[j], quad_ref[...], 0.0), axis=1, keepdims=True
        ) * (1.0 / math.sqrt(quad_ref.shape[1]))
        spread = jnp.where((fold_row % cycles == j) & (fold_col == j), weight, spread)
    spread = spread * (1.0 / math.sqrt(period))
    fold_sum = jnp.concatenate([spread, jnp.where(fold_row < cycles, spread, -spread)], 1)

    def selector(half):
        return jnp.where(fold_row == fold_col + half * cycles, 1.0, 0.0).astype(BF16)

    col = lax.broadcasted_iota(jnp.int32, (set_orders, rows_g), 1) // cycles
    row = lax.broadcasted_iota(jnp.int32, (set_orders, rows_g), 0) % go
    diagonal = row == col

    def pad_rows(at, piece):
        padded[at] = jnp.zeros(padded.shape[1:], BF16)
        both = jnp.concatenate([piece[0].astype(F32), piece[1].astype(F32)], 0)
        padded[at, :, :lon_local] = both.astype(BF16)

    def prepare(s):
        mine = slice(s * set_orders, (s + 1) * set_orders)

        def make_wave(p, carry):
            for q in range(lon_pad // LANES):
                cq = cos_q[p, mine, q : q + 1]
                sq = sin_q[p, mine, q : q + 1]
                cols = slice(q * LANES, (q + 1) * LANES)
                wave[p, s, :set_orders, cols] = (cq * cos_r[mine] - sq * sin_r[mine]).astype(BF16)
                wave[p, s, set_orders:, cols] = (sq * cos_r[mine] + cq * sin_r[mine]).astype(BF16)
            return carry

        lax.fori_loop(0, no, make_wave, 0)
        if s == 0:
            pad_rows(0, press_ref)
            for i, copy in enumerate(press_copies):
                copy.wait()
                pad_rows(i + 1, gathered.at[i])
        sums = jnp.zeros((2 * set_orders, 2 * cycles), F32)
        for i in range(no):
            origin = lax.rem(core + no - i, no)
            sums = sums + lax.dot_general(
                wave[origin, s], padded[i], NT, preferred_element_type=F32
            )
        value = jnp.dot(
            sums, fold_sum, precision=lax.Precision.HIGHEST, preferred_element_type=F32
        )
        for f in range(2):
            half = value[:, f * rows_g : (f + 1) * rows_g]
            lhs[2 * f, mine] = jnp.where(diagonal, half[:set_orders], 0.0)
            lhs[2 * f + 1, mine] = jnp.where(diagonal, -half[set_orders:], 0.0)

    def parity(g, first):
        degree = first + lax.broadcasted_iota(jnp.int32, (go, width), 1)
        order = orders_ref[g * go : (g + 1) * go, :]
        return (degree + order) & 1 == 0, degree >= order

    def region(g, k):
        base = 0
        for at in range(k):
            base = base + ((me // 2 ** orders_of[g][at]) % 2) * (n >> (at + 1))
        return base

    def analyse(g):
        tab_copies[g].wait()
        left = jnp.concatenate([lhs[c, g * go : (g + 1) * go, :] for c in range(4)], 0).astype(BF16)

        def chunk(i, carry):
            first = pl.multiple_of(i * width, width)
            product = jnp.dot(
                left, tab[g * rows_g : (g + 1) * rows_g, pl.ds(first, width)], preferred_element_type=F32
            )
            even, present = parity(g, first)
            real = jnp.where(present, jnp.where(even, product[:go], product[2 * go : 3 * go]), 0.0)
            imag = jnp.where(present, jnp.where(even, product[go : 2 * go], product[3 * go :]), 0.0)
            value = jnp.concatenate([real, imag], 0).astype(BF16)
            for j in range(blocks):
                to = permuted(i * blocks + j, orders_of[g])
                part[g, to] = value[:, j * share : (j + 1) * share]
            return carry

        lax.fori_loop(0, degrees // width, chunk, 0)

    reduce_copies = {}
    gather_copies = {}

    def send_reduce(g, k):
        h = n >> (k + 1)
        b = orders_of[g][k]
        mine = (me // 2**b) % 2
        copy = pltpu.make_async_remote_copy(
            src_ref=part.at[g, pl.ds(region(g, k) + (1 - mine) * h, h)],
            dst_ref=landed.at[g, pl.ds(n - (n >> k), h)],
            send_sem=rs_sem.at[0, g, k],
            recv_sem=rs_sem.at[1, g, k],
            device_id=(partners[b], core),
            device_id_type=MESH,
        )
        copy.start()
        reduce_copies[g, k] = copy

    def take_reduce(g, k):
        h = n >> (k + 1)
        reduce_copies[g, k].wait_recv()
        keep = region(g, k + 1)
        off = n - (n >> k)
        if k < bits - 1:

            def add(i, carry):
                part[g, keep + i] = (
                    part[g, keep + i].astype(F32) + landed[g, off + i].astype(F32)
                ).astype(BF16)
                return carry

            lax.fori_loop(0, h, add, 0, unroll=min(h, 4))
            send_reduce(g, k + 1)
            return
        total = part[g, keep].astype(F32) + landed[g, off].astype(F32)
        spec_ref[0, g * go : (g + 1) * go, :] = total[:go]
        spec_ref[1, g * go : (g + 1) * go, :] = total[go:]
        scaled[g, keep] = (DENSITY_RATIO * (1.0 + love_ref[pl.ds(me, 1), :]) * total).astype(BF16)
        send_gather(g, bits - 1)

    def send_gather(g, k):
        h = n >> (k + 1)
        b = orders_of[g][k]
        mine = pl.ds(region(g, k + 1), h)
        copy = pltpu.make_async_remote_copy(
            src_ref=scaled.at[g, mine],
            dst_ref=scaled.at[g, mine],
            send_sem=ag_sem.at[0, g, k],
            recv_sem=ag_sem.at[1, g, k],
            device_id=(partners[b], core),
            device_id_type=MESH,
        )
        copy.start()
        gather_copies[g, k] = copy

    def take_gather(g, k):
        gather_copies[g, k].wait_recv()
        if k > 0:
            send_gather(g, k - 1)

    def synthesise(g):
        def chunk(i, total):
            first = pl.multiple_of(i * width, width)
            even, _ = parity(g, first)
            pieces = [scaled[g, permuted(i * blocks + j, orders_of[g])] for j in range(blocks)]
            both = jnp.concatenate(pieces, 1).astype(F32)
            real, imag = both[:go], both[go:]
            stacked = jnp.concatenate(
                [real, imag, jnp.where(even, real, -real), jnp.where(even, imag, -imag)], 0
            ).astype(BF16)
            return total + lax.dot_general(
                stacked, tab[g * rows_g : (g + 1) * rows_g, pl.ds(first, width)], NT,
                preferred_element_type=F32,
            )

        total = lax.fori_loop(0, degrees // width, chunk, jnp.zeros((4 * go, rows_g), F32))
        total = total * (1.0 / math.sqrt(degrees))
        keep = diagonal[:go]
        for c in range(4):
            picked[c, g * go : (g + 1) * go, :] = jnp.where(keep, total[c * go : (c + 1) * go], 0.0)

    def synthesise_set(s):
        mine = slice(s * set_orders, (s + 1) * set_orders)
        signal = []
        for t in range(2):
            north, south = [
                lax.dot_general(
                    selector(half), picked[2 * half + t, mine].astype(BF16), NT,
                    preferred_element_type=F32,
                )
                for half in range(2)
            ]
            signal.append(north + south)
        both = jnp.concatenate([signal[0], -signal[1]], 1).astype(BF16)
        for i, peer in enumerate(peers + [core]):
            total = jnp.dot(both, wave[peer, s], preferred_element_type=F32)
            ref = own_piece if i == no - 1 else out_piece.at[i]
            ref[...] = total if s == 0 else ref[...] + total
            if s == SETS - 1 and i < no - 1:
                copy = pltpu.make_async_remote_copy(
                    src_ref=out_piece.at[i],
                    dst_ref=in_piece.at[i],
                    send_sem=field_sem.at[0, i],
                    recv_sem=field_sem.at[1, i],
                    device_id=(me, peer),
                    device_id_type=MESH,
                )
                copy.start()
                field_copies.append(copy)

    field_copies = []
    steps = []
    per_set = GROUPS // SETS
    for s in range(SETS):
        steps.append((s * per_set - 0.5, s, lambda s=s: prepare(s)))
    for g in range(GROUPS):
        steps.append((g, g, lambda g=g: (analyse(g), send_reduce(g, 0))))
        for k in range(bits):
            steps.append((g + STAGGER * (k + 1), g, lambda g=g, k=k: take_reduce(g, k)))
        for i, k in enumerate(reversed(range(bits))):
            steps.append((g + STAGGER * (bits + i + 1), g, lambda g=g, k=k: take_gather(g, k)))
        steps.append((g + STAGGER * 2 * bits + 0.5, g, lambda g=g: synthesise(g)))
    for s in range(SETS):
        last = (s + 1) * per_set - 1
        steps.append((last + STAGGER * 2 * bits + 0.75, s, lambda s=s: synthesise_set(s)))
    for _, _, step in sorted(steps, key=lambda s: (s[0], s[1])):
        step()

    total = own_piece[...]
    for i, copy in enumerate(field_copies):
        copy.wait_recv()
        total = total + in_piece[i]
    total = total[:, :lon_local] * (1.0 / math.sqrt(local_orders * no))
    field_ref[0] = total[:cycles]
    field_ref[1] = total[cycles:]
    for copy in list(reduce_copies.values()) + list(gather_copies.values()) + field_copies:
        copy.wait_send()


def per_device(n, no, pressure, tables, quad_weight, love_number, order_list, cycle_list):
    _, cycles, lon_local = pressure.shape
    local_orders, _, degrees = tables.shape
    bits = n.bit_length() - 1
    share = degrees // n
    go = local_orders // GROUPS
    rows_g = go * cycles
    lon_pad = -(-lon_local // LANES) * LANES
    vmem = pl.BlockSpec(memory_space=pltpu.VMEM)
    table = pltpu.VMEM((local_orders, LANES), F32)
    tables_q = pltpu.VMEM((no, local_orders, LANES), F32)
    blocks = pltpu.VMEM((GROUPS, n, 2 * go, share), BF16)
    pieces = pltpu.VMEM((no - 1, 2 * cycles, lon_pad), F32)
    return pl.pallas_call(
        functools.partial(kernel, n, no),
        out_shape=(
            jax.ShapeDtypeStruct((2, local_orders, share), F32),
            jax.ShapeDtypeStruct((2, cycles, lon_local), F32),
        ),
        in_specs=[
            vmem, pl.BlockSpec(memory_space=pl.ANY), vmem, vmem, vmem,
            pl.BlockSpec(memory_space=pltpu.SMEM),
        ],
        out_specs=(vmem, vmem),
        scratch_shapes=[
            pltpu.VMEM((local_orders * cycles, degrees), BF16),
            pltpu.VMEM((no, SETS, 2 * local_orders // SETS, lon_pad), BF16),
            pltpu.VMEM((no - 1, 2, cycles, lon_local), BF16),
            pltpu.VMEM((no, 2 * cycles, lon_pad), BF16),
            tables_q, tables_q, table, table,
            pltpu.VMEM((local_orders, 1), jnp.int32),
            pltpu.VMEM((4, local_orders, rows_g), F32),
            blocks, blocks, blocks,
            pltpu.VMEM((4, local_orders, rows_g), F32),
            pltpu.VMEM((2 * cycles, lon_pad), F32),
            pieces, pieces,
            pltpu.SemaphoreType.DMA((GROUPS,)),
            pltpu.SemaphoreType.DMA((2, no - 1)),
            pltpu.SemaphoreType.DMA((2, GROUPS, bits)),
            pltpu.SemaphoreType.DMA((2, GROUPS, bits)),
            pltpu.SemaphoreType.DMA((2, no - 1)),
        ],
        compiler_params=pltpu.CompilerParams(
            collective_id=0, has_side_effects=True, vmem_limit_bytes=56 * 1024 * 1024
        ),
    )(
        pressure, tables.reshape(local_orders * cycles, degrees), quad_weight[None, :],
        love_number.reshape(n, share), order_list[None, :], cycle_list,
    )


def solution(mesh):
    placed = (P(None, "lat", "ord"), P("ord", "lat", None), P(), P(), P(), P("lat"))
    return jax.shard_map(
        functools.partial(per_device, mesh.shape["lat"], mesh.shape["ord"]),
        mesh=mesh,
        in_specs=placed,
        out_specs=(P(None, "ord", "lat"), P(None, "lat", "ord")),
        check_vma=False,
    )
```

time: 81.5 us -> 64.6 us (0.79)
  other arithmetic: 6.84 us -> 0 us
  Pallas kernels: 67.2 us -> 60.5 us
  local copies, waits for them, and re-layouts: 6.5 us -> 3.28 us
    pallas_call x1, Pallas kernels: 67.2 us -> 60.5 us  [per_device(): pl.pallas_call(functools.partial(kernel, n, no), out_shape=(jax.ShapeDtyp...]
    sin x2 -> x0, other arithmetic: 3.3 us -> none  [cos_sin(): return (jnp.cos(angle), jnp.sin(angle))]
    pad x1 -> x0, local copies, waits for them, and re-layouts: 1.54 us -> none  [per_device(): jnp.pad(pressure.reshape(2 * cycles, lon_local), ((0, 0), (0, lon_pad - l...]
    dynamic_slice x1 -> x0, other arithmetic: 1.27 us -> none  [per_device(): lax.dynamic_slice_in_dim(love, lax.axis_index('lat') * share, share, 1)]
    another operation x3 -> x0, other arithmetic: 1.25 us -> none  [the longest x2 0.63 us: per_device(): jnp.stack([jnp.concatenate([spread, spread], 0), -jnp.concatenate([spread...]
    reduce_sum x1 -> x0, other arithmetic: 0.85 us -> none  [per_device(): jnp.sum(jnp.where(matches, quad_weight[None, :], 0.0), axis=1)]
where the time goes in v1:
time: 64.6 us; the launch traced here: 64.4 us
  Pallas kernels  60.5 us (94%)
  local copies, waits for them, and re-layouts  3.28 us (5%)
    pallas_call x1, Pallas kernels, per_device(): pl.pallas_call(functools.partial(kernel, n, no), out_shape=(jax.ShapeDtyp...  60.5 us
    unnamed x2, local copies, waits for them, and re-layouts  3.28 us

profile of v1, /device:TPU:0, one launch (start us, length us, event | category | flops | bytes accessed | tf_op | source)
XLA Modules:
  0.0 64.4 jit_solution(2590982434310907518)
XLA Ops:
  0.6 60.5 %shard_map.77 = (f32[2,256,128]{2,1,0:T(8,128)}, f32[2,8,2880]{2,1,0:T(8,128)}) custom-call(bf16[2,8,2880]{2,1,0:T(8,128)(2,1)} %press_ref.1, bf16[2048,2048]{1,0:T(8,128)(2,1)} %bitcast.4, f32[1,128]{1,0:T(1,128)} %bitcast.7, f32[16,128]{1,0:T(8,128)} %bitcast.5, s32[1,512]{1,0:T(1,128)} %bitcast.6, s32[8]{0:T(128)} %cycle_ref.1), custom_call_target="tpu_custom_call" | custom-call | tf_op jit(solution)/shard_map/pallas_call | solution.py:363
  61.2 1.7 %copy.10 = f32[2,256,128]{2,1,0:T(8,128)} copy(f32[2,256,128]{2,1,0:T(8,128)} %get-tuple-element.4) | data formatting | bytes 524288
  62.8 1.6 %copy.11 = f32[2,8,2880]{2,1,0:T(8,128)} copy(f32[2,8,2880]{2,1,0:T(8,128)} %get-tuple-element.5) | data formatting | bytes 368640

commit v2 on v1

--- a/solution.py
+++ b/solution.py
@@ -11,7 +11,7 @@
 DENSITY_RATIO = 3.0 * 1025.0 / 5517.0
 LANES = 128
 GROUPS = 8
-SETS = 2
+SETS = 4
 STAGGER = 4
 MESH = pl.DeviceIdType.MESH
 NT = (((1,), (1,)), ((), ()))
@@ -27,7 +27,9 @@
     b = [1, 0] + base[2:]
     c = [2, 0, 1] + base[3:]
     d = [2, 1, 0] + base[3:]
-    return [a, b, c, a, b, d, a, b]
+    e = [0, 2, 1] + base[3:]
+    f = [1, 2, 0] + base[3:]
+    return [a, b, c, e, f, d, a, b]
 
 
 def permuted(index, order):
@@ -55,7 +57,7 @@
 def kernel(
     n, no,
     press_ref, tables_ref, quad_ref, love_ref, order_ref, cycle_ref,
-    spec_ref, field_ref,
+    spec_ref, total_ref,
     tab, wave, gathered, padded, cos_q, sin_q, cos_r, sin_r, orders_ref, lhs, part, landed, scaled,
     picked, own_piece, out_piece, in_piece,
     tab_sem, press_sem, rs_sem, ag_sem, field_sem,
@@ -336,15 +338,20 @@
     for _, _, step in sorted(steps, key=lambda s: (s[0], s[1])):
         step()
 
-    total = own_piece[...]
-    for i, copy in enumerate(field_copies):
+    for copy in field_copies:
         copy.wait_recv()
-        total = total + in_piece[i]
-    total = total[:, :lon_local] * (1.0 / math.sqrt(local_orders * no))
-    field_ref[0] = total[:cycles]
-    field_ref[1] = total[cycles:]
+    total_ref[...] = own_piece[...]
+    for i in range(no - 1):
+        total_ref[...] += in_piece[i]
     for copy in list(reduce_copies.values()) + list(gather_copies.values()) + field_copies:
         copy.wait_send()
+
+
+def finish(scale, half_spec, total_ref, spec_ref, field_ref):
+    cycles, lon_local = field_ref.shape[1:]
+    spec_ref[...] = half_spec[...]
+    for h in range(2):
+        field_ref[h] = total_ref[h * cycles : (h + 1) * cycles, :lon_local] * scale
 
 
 def per_device(n, no, pressure, tables, quad_weight, love_number, order_list, cycle_list):
@@ -360,11 +367,11 @@
     tables_q = pltpu.VMEM((no, local_orders, LANES), F32)
     blocks = pltpu.VMEM((GROUPS, n, 2 * go, share), BF16)
     pieces = pltpu.VMEM((no - 1, 2 * cycles, lon_pad), F32)
-    return pl.pallas_call(
+    spectrum, total = pl.pallas_call(
         functools.partial(kernel, n, no),
         out_shape=(
             jax.ShapeDtypeStruct((2, local_orders, share), F32),
-            jax.ShapeDtypeStruct((2, cycles, lon_local), F32),
+            jax.ShapeDtypeStruct((2 * cycles, lon_pad), F32),
         ),
         in_specs=[
             vmem, pl.BlockSpec(memory_space=pl.ANY), vmem, vmem, vmem,
@@ -396,6 +403,15 @@
         pressure, tables.reshape(local_orders * cycles, degrees), quad_weight[None, :],
         love_number.reshape(n, share), order_list[None, :], cycle_list,
     )
+    return pl.pallas_call(
+        functools.partial(finish, 1.0 / math.sqrt(local_orders * no)),
+        out_shape=(
+            jax.ShapeDtypeStruct(spectrum.shape, F32),
+            jax.ShapeDtypeStruct((2, cycles, lon_local), F32),
+        ),
+        in_specs=[vmem, vmem],
+        out_specs=(vmem, vmem),
+    )(spectrum, total)
 
 
 def solution(mesh):

time: 64.6 us -> 60 us (0.929)
  local copies, waits for them, and re-layouts: 3.28 us -> 0 us
  Pallas kernels: 60.5 us -> 59.2 us
    unnamed x2 -> x0, local copies, waits for them, and re-layouts: 3.28 us -> none
    pallas_call x1, Pallas kernels: 60.5 us -> 57.4 us  [per_device(): pl.pallas_call(functools.partial(kernel, n, no), out_shape=(jax.ShapeDtyp...]
    pallas_call x0 -> x1, Pallas kernels: none -> 1.78 us  [per_device(): pl.pallas_call(functools.partial(finish, 1.0 / math.sqrt(local_orders * n...]
where the time goes in v2:
time: 60 us; the launch traced here: 59.8 us
  Pallas kernels  59.2 us (99%)
  between operations  0.64 us (1%)
    pallas_call x1, Pallas kernels, per_device(): pl.pallas_call(functools.partial(kernel, n, no), out_shape=(jax.ShapeDtyp...  57.4 us
    pallas_call x1, Pallas kernels, per_device(): pl.pallas_call(functools.partial(finish, 1.0 / math.sqrt(local_orders * n...  1.78 us

profile of v2, /device:TPU:0, one launch (start us, length us, event | category | flops | bytes accessed | tf_op | source)
XLA Modules:
  0.0 59.8 jit_solution(15796676221784260892)
XLA Ops:
  0.6 57.4 %shard_map.77 = (f32[2,256,128]{2,1,0:T(8,128)}, f32[16,2944]{1,0:T(8,128)}) custom-call(bf16[2,8,2880]{2,1,0:T(8,128)(2,1)} %press_ref.1, bf16[2048,2048]{1,0:T(8,128)(2,1)} %bitcast.4, f32[1,128]{1,0:T(1,128)} %bitcast.7, f32[16,128]{1,0:T(8,128)} %bitcast.5, s32[1,512]{1,0:T(1,128)} %bitcast.6, s32[8]{0:T(128)} %cycle_ref.1), custom_call_target="tpu_custom_call" | custom-call | tf_op jit(solution)/shard_map/pallas_call | solution.py:370
  58.0 1.8 %shard_map.78 = (f32[2,256,128]{2,1,0:T(8,128)}, f32[2,8,2880]{2,1,0:T(8,128)}) custom-call(f32[2,256,128]{2,1,0:T(8,128)} %get-tuple-element.4.half_spec, f32[16,2944]{1,0:T(8,128)} %get-tuple-element.5.total_ref), custom_call_target="tpu_custom_call" | custom-call | tf_op jit(solution)/shard_map/pallas_call | solution.py:406
